TPU v7x, 256 devices: a 8x8x2 block of a 8x8x16 slice. The times are simulated.
256 devices in a mesh: groups: 2 (over z), rows: 16 (over y, core), cols: 8 (over x).
Axes of the slice: x: 8, y: 8, z: 2, core: 2. Of those that a mesh axis runs over, the one named last changes fastest.
The devices are a block of a 8x8x16 slice.
Arguments:
- pair_state: float32 [768, 384, 128], P(('groups', 'rows'), 'cols'), parts along dimension 0, may hold values from -6 to 6
- token_mask: int32 [768], P('groups'), parts along dimension 0, may hold values 0 or 1
- norm_gain: float32 [2, 128], replicated, may hold values from 0.25 to 1.75
- norm_bias: float32 [2, 128], replicated, may hold values from -3 to 3
- proj_weight: float32 [2, 128, 512], replicated, may hold values from -0.5 to 0.5
- gate_weight: float32 [2, 128, 128], replicated, may hold values from -0.5 to 0.5
- out_gain: float32 [2, 128], replicated, may hold values from 0.25 to 1.75
- out_bias: float32 [2, 128], replicated, may hold values from -3 to 3
- out_weight: float32 [2, 128, 128], replicated, may hold values from -0.5 to 0.5
Outputs:
- pair_out: float32 [768, 384, 128], P(('groups', 'rows'), 'cols'), parts along dimension 0
There are 2 independent parts, one for each index of `groups`. A program takes and returns all parts, laid end to end along the dimension named above; an argument that names none is the same for every part. Nothing has to cross between parts.
All inputs are finite; a program needn't handle non-finite values.
Results may differ from a plain program's by a relative error of at most 0.0001.
Values sent between devices are 32-bit elements; how exact they have to be, the bound alone decides.
A program may use at most 128 MiB of HBM per device.

v0:
```python
import jax
import jax.numpy as jnp
from jax import lax
from jax.sharding import PartitionSpec as P

eps = 1e-05


def normalize(values, gain, shift):
    center = values - jnp.mean(values, axis=-1, keepdims=True)
    spread = jnp.mean(center * center, axis=-1, keepdims=True)
    return center * lax.rsqrt(spread + eps) * gain + shift


def project(state, pair_mask, segment, norm_gain, norm_bias, proj_weight, gate_weight):
    width = proj_weight.shape[2] // 4
    normed = normalize(state, norm_gain[segment], norm_bias[segment])
    hidden = jnp.einsum(
        "ijc,cf->ijf", normed, proj_weight[segment], precision=lax.Precision.HIGHEST
    )
    left_side = (
        pair_mask[:, :, None]
        * jax.nn.sigmoid(hidden[:, :, :width])
        * hidden[:, :, width : 2 * width]
    )
    right_side = (
        pair_mask[:, :, None]
        * jax.nn.sigmoid(hidden[:, :, 2 * width : 3 * width])
        * hidden[:, :, 3 * width :]
    )
    gating = jax.nn.sigmoid(
        jnp.einsum("ijc,cd->ijd", normed, gate_weight[segment], precision=lax.Precision.HIGHEST)
    )
    return (left_side, right_side, gating)


def finish(state, mixed, gating, segment, out_gain, out_bias, out_weight):
    result = jnp.einsum(
        "ijh,hc->ijc",
        normalize(mixed, out_gain[segment], out_bias[segment]),
        out_weight[segment],
        precision=lax.Precision.HIGHEST,
    )
    return state + gating * result


def body(
    pair_state,
    token_mask,
    norm_gain,
    norm_bias,
    proj_weight,
    gate_weight,
    out_gain,
    out_bias,
    out_weight,
):
    row_count = pair_state.shape[0]
    col_count = pair_state.shape[1]
    row_start = lax.axis_index("rows") * row_count
    col_start = lax.axis_index("cols") * col_count
    maskf = token_mask.astype(jnp.float32)
    row_mask = lax.dynamic_slice_in_dim(maskf, row_start, row_count)
    col_mask = lax.dynamic_slice_in_dim(maskf, col_start, col_count)
    pair_mask = row_mask[:, None] * col_mask[None, :]
    left_side, right_side, gating = project(
        pair_state, pair_mask, 0, norm_gain, norm_bias, proj_weight, gate_weight
    )
    partial_out = jnp.einsum(
        "ikh,jkh->ijh",
        left_side,
        lax.all_gather(right_side, "rows", axis=0, tiled=True),
        precision=lax.Precision.HIGHEST,
    )
    mixed = lax.psum_scatter(partial_out, "cols", scatter_dimension=1, tiled=True)
    updated = finish(pair_state, mixed, gating, 0, out_gain, out_bias, out_weight)
    left_next, right_next, gate_next = project(
        updated, pair_mask, 1, norm_gain, norm_bias, proj_weight, gate_weight
    )
    partial_in = jnp.einsum(
        "kih,kjh->ijh",
        lax.all_gather(left_next, "cols", axis=1, tiled=True),
        right_next,
        precision=lax.Precision.HIGHEST,
    )
    mixed_next = lax.psum_scatter(partial_in, "rows", scatter_dimension=0, tiled=True)
    return finish(updated, mixed_next, gate_next, 1, out_gain, out_bias, out_weight)


def solution(mesh):
    placed = (P(("groups", "rows"), "cols", None), P("groups"), P(), P(), P(), P(), P(), P(), P())
    return jax.shard_map(
        body,
        mesh=mesh,
        in_specs=placed,
        out_specs=P(("groups", "rows"), "cols", None),
        check_vma=False,
    )
```

profile of v0, /device:TPU:514, one launch (start us, length us, event | category | flops | bytes accessed | tf_op | source)
XLA Modules:
  0.0 397.2 jit_solution(2512777455134591097)
XLA Ops:
  6.6 0.7 convert_element_type.3
  7.2 0.1 dynamic_slice.6
  7.3 0.1 dynamic_slice.7
  7.4 1.3 reduce_sum.72
  8.7 1.5 multiply_reduce_fusion.3
  10.2 0.1 broadcast_multiply_fusion
  10.3 0.8 slice_bitcast_fusion.2
  11.0 3.2 fusion.29
  14.2 1.2 slice_multiply_fusion.2
  15.4 0.1 all-gather.3.cloned.1.call-update
  15.4 0.1 reduce-scatter.3.cloned.1.call-start
  15.5 0.5 copy.47
  16.1 79.5 %all-gather.3.cloned.1.call-done = f32[384,48,128]{2,1,0:T(8,128)} async-done(((f32[24,48,128]{2,1,0:T(8,128)}), f32[384,48,128]{2,1,0:T(8,128)}) %all-gather.3.cloned.1.call-update) | async-done | bytes 9437200 | tf_op jit(solution)/shard_map/all_gather | solution.py:72
  95.6 21.7 %copy.46 = f32[384,48,128]{1,0,2:T(8,128)} copy(f32[384,48,128]{2,1,0:T(8,128)} %all-gather.3.cloned.1.call-done) | data formatting | bytes 18874368 | tf_op jit(solution)/shard_map/all_gather | solution.py:72
  117.3 31.6 %convolution_bitcast_fusion.1 = f32[24,384,128]{1,0,2:T(8,128)} fusion(f32[384,48,128]{1,0,2:T(8,128)} %copy.46, f32[24,48,128]{1,0,2:T(8,128)S(1)} %copy.47), kind=kOutput, calls=%fused_computation.1 | convolution fusion | flops 679477248 | bytes 14745600 | tf_op jit(solution)/shard_map/ikh,jkh->ijh/dot_general | solution.py:69
  148.9 6.0 %copy.48 = f32[24,384,128]{2,0,1:T(8,128)} copy(f32[24,384,128]{1,0,2:T(8,128)} %convolution_bitcast_fusion.1) | data formatting | bytes 9437184 | tf_op jit(solution)/shard_map/ikh,jkh->ijh/transpose | solution.py:69
  154.9 0.1 reduce-scatter.3.cloned.1.call-update
  155.0 0.2 all-gather.5.cloned.1.call-start
  155.2 0.3 copy-done.3
  155.6 0.0 copy-done.4
  155.6 0.4 copy-done
  156.0 0.0 copy-done.5
  156.0 0.8 fusion.7
  156.8 56.9 %reduce-scatter.3.cloned.1.call-done = f32[24,48,128]{2,0,1:T(8,128)} async-done(((f32[24,384,128]{2,0,1:T(8,128)}), f32[24,48,128]{2,0,1:T(8,128)}) %reduce-scatter.3.cloned.1.call-update) | async-done | bytes 589840 | tf_op jit(solution)/shard_map/reduce_scatter | solution.py:75
  213.7 1.3 reduce_sum.74
  215.0 0.1 copy.49
  215.1 0.1 copy.50
  215.2 1.5 multiply_reduce_fusion.2
  216.6 0.1 copy.51
  216.7 0.1 copy.52
  216.8 1.4 multiply_add_fusion.1
  218.3 0.7 fusion.63
  219.0 0.4 multiply_reduce_fusion.1
  219.4 2.1 fusion.30
  221.5 1.2 slice_multiply_fusion
  222.6 0.1 all-gather.5.cloned.1.call-update
  222.7 0.1 reduce-scatter.5.cloned.1.call-start
  222.8 0.5 copy.54
  223.3 59.2 %all-gather.5.cloned.1.call-done = f32[24,384,128]{2,1,0:T(8,128)} async-done(((f32[24,48,128]{2,1,0:T(8,128)}), f32[24,384,128]{2,1,0:T(8,128)}) %all-gather.5.cloned.1.call-update) | async-done | bytes 4718608 | tf_op jit(solution)/shard_map/all_gather | solution.py:82
  282.6 6.2 %copy.55 = f32[24,384,128]{1,0,2:T(8,128)} copy(f32[24,384,128]{2,1,0:T(8,128)} %all-gather.5.cloned.1.call-done) | data formatting | bytes 9437184 | tf_op jit(solution)/shard_map/all_gather | solution.py:82
  288.8 11.8 %convolution_bitcast_fusion = f32[384,48,128]{0,1,2:T(8,128)} fusion(f32[24,48,128]{1,0,2:T(8,128)S(1)} %copy.54, f32[24,384,128]{1,0,2:T(8,128)} %copy.55), kind=kOutput, calls=%fused_computation | convolution fusion | flops 679477248 | bytes 14745600 | tf_op jit(solution)/shard_map/kih,kjh->ijh/dot_general | solution.py:80
  300.5 9.8 %copy.56 = f32[384,48,128]{2,1,0:T(8,128)} copy(f32[384,48,128]{0,1,2:T(8,128)} %convolution_bitcast_fusion) | data formatting | bytes 18874368 | tf_op jit(solution)/shard_map/kih,kjh->ijh/transpose | solution.py:80
  310.3 0.1 reduce-scatter.5.cloned.1.call-update
  310.4 0.8 fusion.3
  311.2 74.0 %reduce-scatter.5.cloned.1.call-done = f32[24,48,128]{2,1,0:T(8,128)} async-done(((f32[384,48,128]{2,1,0:T(8,128)}), f32[24,48,128]{2,1,0:T(8,128)}) %reduce-scatter.5.cloned.1.call-update) | async-done | bytes 589840 | tf_op jit(solution)/shard_map/reduce_scatter | solution.py:86
  385.2 1.3 reduce_sum.78
  386.5 1.5 multiply_reduce_fusion
  388.0 2.7 fusion
  (18 shorter events, 0.1 us)
Async XLA Ops:
  6.5 89.1 %all-gather.3.cloned.1.call-start = ((), (), s32[]{:S(2)}) async-start(), calls=%async_computation.2 | async-start | bytes 10027008 | tf_op jit(solution)/shard_map/all_gather | solution.py:72
  15.4 198.3 %reduce-scatter.3.cloned.1.call-start = ((), (), s32[]{:S(2)}) async-start(), calls=%async_computation.3 | async-start | bytes 5308416 | tf_op jit(solution)/shard_map/reduce_scatter | solution.py:75
  154.9 0.7 copy-start.3
  154.9 0.7 copy-start.4
  154.9 1.1 copy-start
  154.9 1.1 copy-start.5
  154.9 63.3 %copy-start.2 = (f32[2,128,128]{2,1,0:T(8,128)S(1)}, f32[2,128,128]{2,1,0:T(8,128)}, u32[]{:S(2)}) copy-start(f32[2,128,128]{2,1,0:T(8,128)} %param.17) | copy-start | bytes 393220
  155.0 64.4 %copy-start.1 = (f32[2,128,512]{2,1,0:T(8,128)S(1)}, f32[2,128,512]{2,1,0:T(8,128)}, u32[]{:S(2)}) copy-start(f32[2,128,512]{2,1,0:T(8,128)} %param.13) | copy-start | bytes 1572868
  155.0 127.6 %all-gather.5.cloned.1.call-start = ((), (), s32[]{:S(2)}) async-start(), calls=%async_computation.4 | async-start | bytes 5308416 | tf_op jit(solution)/shard_map/all_gather | solution.py:82
  222.7 162.5 %reduce-scatter.5.cloned.1.call-start = ((), (), s32[]{:S(2)}) async-start(), calls=%async_computation.5 | async-start | bytes 10027008 | tf_op jit(solution)/shard_map/reduce_scatter | solution.py:86
Sparse Core Ops, SparseCore 0:
  15.6 79.9 all-gather.2
  155.1 58.5 reduce-scatter.2
  222.8 59.6 all-gather.4
  310.5 74.6 reduce-scatter.4
where the time goes:
time: 398 us; the launch traced here: 397 us
  waiting for transfers between devices  270 us (68%)
  matrix products  53.6 us (13%)
  local copies, waits for them, and re-layouts  46.8 us (12%)
  other arithmetic  13.3 us (3%)
  between operations  13.3 us (3%)
    all_gather x1, waiting for transfers between devices, body(): lax.all_gather(right_side, 'rows', axis=0, tiled=True)  79.5 us
    reduce_scatter x1, waiting for transfers between devices, body(): lax.psum_scatter(partial_in, 'rows', scatter_dimension=0, tiled=True)  74 us
    all_gather x1, waiting for transfers between devices, body(): lax.all_gather(left_next, 'cols', axis=1, tiled=True)  59.2 us
    reduce_scatter x1, waiting for transfers between devices, body(): lax.psum_scatter(partial_out, 'cols', scatter_dimension=1, tiled=True)  56.9 us
    dot_general x1, matrix products, body(): jnp.einsum('ikh,jkh->ijh', left_side, lax.all_gather(right_side, 'rows',...  31.6 us
    all_gather x1, local copies, waits for them, and re-layouts, body(): lax.all_gather(right_side, 'rows', axis=0, tiled=True)  21.7 us
    dot_general x1, matrix products, body(): jnp.einsum('kih,kjh->ijh', lax.all_gather(left_next, 'cols', axis=1, tile...  11.8 us
    transpose x1, local copies, waits for them, and re-layouts, body(): jnp.einsum('kih,kjh->ijh', lax.all_gather(left_next, 'cols', axis=1, tile...  9.8 us
  transfers between devices with their start and end apart: 4, of which 4 were waited for; matrix products, arithmetic and copies ran while one was open for 1% of the time, Pallas kernels for 0%

commit v1 on v0

--- a/solution.py
+++ b/solution.py
@@ -66,11 +66,15 @@
     left_side, right_side, gating = project(
         pair_state, pair_mask, 0, norm_gain, norm_bias, proj_weight, gate_weight
     )
+
+    def _draw_squares(u_in):
+        inbox = []
+        for _ in range(lax.axis_size("rows")):
+            inbox.append(u_in)
+        return jnp.concatenate(lax.all_to_all(jnp.stack(inbox), "rows", 0, 0), axis=0)
+
     partial_out = jnp.einsum(
-        "ikh,jkh->ijh",
-        left_side,
-        lax.all_gather(right_side, "rows", axis=0, tiled=True),
-        precision=lax.Precision.HIGHEST,
+        "ikh,jkh->ijh", left_side, _draw_squares(right_side), precision=lax.Precision.HIGHEST
     )
     mixed = lax.psum_scatter(partial_out, "cols", scatter_dimension=1, tiled=True)
     updated = finish(pair_state, mixed, gating, 0, out_gain, out_bias, out_weight)

time: 398 us -> 519 us (1.30)
  waiting for transfers between devices: 270 us -> 407 us
  matrix products: 53.6 us -> 31.9 us
  starting transfers between devices: 0.38 us -> 14.1 us
  local copies, waits for them, and re-layouts: 46.8 us -> 39.5 us
    all_to_all x0 -> x1, waiting for transfers between devices: none -> 206 us  [_draw_squares(): lax.all_to_all(jnp.stack(inbox), 'rows', 0, 0)]
    all_gather x1 -> x0, waiting for transfers between devices: 79.5 us -> none  [body(): lax.all_gather(right_side, 'rows', axis=0, tiled=True)]
    dot_general x1, matrix products: 31.6 us -> 9.88 us  [body(): jnp.einsum('ikh,jkh->ijh', left_side, _draw_squares(right_side), precisio...]
    all_gather x1 -> x0, local copies, waits for them, and re-layouts: 21.7 us -> none  [body(): lax.all_gather(right_side, 'rows', axis=0, tiled=True)]
    all_to_all x0 -> x1, starting transfers between devices: none -> 13.5 us  [_draw_squares(): lax.all_to_all(jnp.stack(inbox), 'rows', 0, 0)]
    reduce_scatter x1, waiting for transfers between devices: 56.9 us -> 67.5 us  [body(): lax.psum_scatter(partial_out, 'cols', scatter_dimension=1, tiled=True)]
    reshape x0 -> x1, local copies, waits for them, and re-layouts: none -> 9.76 us  [_draw_squares(): jnp.concatenate(lax.all_to_all(jnp.stack(inbox), 'rows', 0, 0), axis=0)]
where the time goes in v1:
time: 519 us; the launch traced here: 518 us
  waiting for transfers between devices  407 us (78%)
  local copies, waits for them, and re-layouts  39.5 us (8%)
  matrix products  31.9 us (6%)
  starting transfers between devices  14.1 us (3%)
  between operations  13.3 us (3%)
  other arithmetic  12.5 us (2%)
    all_to_all x1, waiting for transfers between devices, _draw_squares(): lax.all_to_all(jnp.stack(inbox), 'rows', 0, 0)  206 us
    reduce_scatter x1, waiting for transfers between devices, body(): lax.psum_scatter(partial_in, 'rows', scatter_dimension=0, tiled=True)  73.9 us
    reduce_scatter x1, waiting for transfers between devices, body(): lax.psum_scatter(partial_out, 'cols', scatter_dimension=1, tiled=True)  67.5 us
    all_gather x1, waiting for transfers between devices, body(): lax.all_gather(left_next, 'cols', axis=1, tiled=True)  59 us
    all_to_all x1, starting transfers between devices, _draw_squares(): lax.all_to_all(jnp.stack(inbox), 'rows', 0, 0)  13.5 us
    dot_general x1, matrix products, body(): jnp.einsum('kih,kjh->ijh', lax.all_gather(left_next, 'cols', axis=1, tile...  11.8 us
  transfers between devices with their start and end apart: 4, of which 4 were waited for; matrix products, arithmetic and copies ran while one was open for 1% of the time, Pallas kernels for 0%

profile of v1, /device:TPU:514, one launch (start us, length us, event | category | flops | bytes accessed | tf_op | source)
XLA Modules:
  0.0 517.8 jit_solution(15215196038824469978)
XLA Ops:
  6.5 0.7 convert_element_type.3
  7.2 0.1 dynamic_slice.6
  7.3 0.1 dynamic_slice.7
  7.4 1.3 reduce_sum.72
  8.7 1.5 multiply_reduce_fusion.3
  10.2 0.1 broadcast_multiply_fusion
  10.3 0.8 slice_bitcast_fusion.2
  11.0 3.2 fusion.29
  14.2 0.3 slice_multiply_fusion.2
  14.6 4.6 stack.2
  19.1 13.5 %all-to-all-start = ((f32[16,24,48,128]{3,2,1,0:T(8,128)}), f32[16,24,48,128]{3,2,1,0:T(8,128)}, u32[]{:S(2)}, u32[]{:S(2)}) async-start(f32[16,24,48,128]{3,2,1,0:T(8,128)} %stack.2), calls=%async_computation | async-start | bytes 18874368 | tf_op jit(solution)/shard_map/all_to_all | solution.py:74
  32.6 0.1 reduce-scatter.3.cloned.1.call-start
  32.7 0.5 copy.55
  33.2 205.9 %all-to-all-done = f32[16,24,48,128]{3,2,1,0:T(8,128)} async-done(((f32[16,24,48,128]{3,2,1,0:T(8,128)}), f32[16,24,48,128]{3,2,1,0:T(8,128)}, u32[]{:S(2)}, u32[]{:S(2)}) %all-to-all-start) | async-done | bytes 9437216 | tf_op jit(solution)/shard_map/all_to_all | solution.py:74
  239.1 9.8 %copy.54 = f32[384,48,128]{0,1,2:T(8,128)} copy(f32[384,48,128]{2,1,0:T(8,128)} %bitcast.6) | data formatting | bytes 18874368 | tf_op jit(solution)/shard_map/reshape | solution.py:74
  248.9 9.9 %convolution_bitcast_fusion.1 = f32[24,384,128]{1,0,2:T(8,128)} fusion(f32[384,48,128]{0,1,2:T(8,128)} %copy.54, f32[24,48,128]{1,0,2:T(8,128)S(1)} %copy.55), kind=kOutput, calls=%fused_computation.1 | convolution fusion | flops 679477248 | bytes 14745600 | tf_op jit(solution)/shard_map/ikh,jkh->ijh/dot_general | solution.py:76
  258.7 6.1 %copy.56 = f32[24,384,128]{2,0,1:T(8,128)} copy(f32[24,384,128]{1,0,2:T(8,128)} %convolution_bitcast_fusion.1) | data formatting | bytes 9437184 | tf_op jit(solution)/shard_map/ikh,jkh->ijh/transpose | solution.py:76
  264.9 0.1 reduce-scatter.3.cloned.1.call-update
  265.0 0.2 all-gather.2.cloned.1.call-start
  265.2 0.3 copy-done.3
  265.6 0.4 copy-done
  266.0 0.0 copy-done.5
  266.0 0.8 fusion.7
  266.8 67.5 %reduce-scatter.3.cloned.1.call-done = f32[24,48,128]{2,0,1:T(8,128)} async-done(((f32[24,384,128]{2,0,1:T(8,128)}), f32[24,48,128]{2,0,1:T(8,128)}) %reduce-scatter.3.cloned.1.call-update) | async-done | bytes 589840 | tf_op jit(solution)/shard_map/reduce_scatter | solution.py:79
  334.4 1.3 reduce_sum.74
  335.6 0.1 copy.57
  335.7 0.1 copy.58
  335.8 1.5 multiply_reduce_fusion.2
  337.3 0.1 copy.59
  337.4 0.1 copy.60
  337.4 1.4 multiply_add_fusion.1
  338.9 0.7 fusion.63
  339.6 0.4 multiply_reduce_fusion.1
  340.1 2.1 fusion.30
  342.1 1.2 slice_multiply_fusion
  343.3 0.1 all-gather.2.cloned.1.call-update
  343.3 0.3 reduce-scatter.5.cloned.1.call-start
  343.6 0.5 copy.62
  344.2 59.0 %all-gather.2.cloned.1.call-done = f32[24,384,128]{2,1,0:T(8,128)} async-done(((f32[24,48,128]{2,1,0:T(8,128)}), f32[24,384,128]{2,1,0:T(8,128)}) %all-gather.2.cloned.1.call-update) | async-done | bytes 4718608 | tf_op jit(solution)/shard_map/all_gather | solution.py:86
  403.2 6.2 %copy.63 = f32[24,384,128]{1,0,2:T(8,128)} copy(f32[24,384,128]{2,1,0:T(8,128)} %all-gather.2.cloned.1.call-done) | data formatting | bytes 9437184 | tf_op jit(solution)/shard_map/all_gather | solution.py:86
  409.4 11.8 %convolution_bitcast_fusion = f32[384,48,128]{0,1,2:T(8,128)} fusion(f32[24,48,128]{1,0,2:T(8,128)S(1)} %copy.62, f32[24,384,128]{1,0,2:T(8,128)} %copy.63), kind=kOutput, calls=%fused_computation | convolution fusion | flops 679477248 | bytes 14745600 | tf_op jit(solution)/shard_map/kih,kjh->ijh/dot_general | solution.py:84
  421.2 9.8 %copy.64 = f32[384,48,128]{2,1,0:T(8,128)} copy(f32[384,48,128]{0,1,2:T(8,128)} %convolution_bitcast_fusion) | data formatting | bytes 18874368 | tf_op jit(solution)/shard_map/kih,kjh->ijh/transpose | solution.py:84
  431.0 0.1 reduce-scatter.5.cloned.1.call-update
  431.0 0.8 fusion.3
  431.9 73.9 %reduce-scatter.5.cloned.1.call-done = f32[24,48,128]{2,1,0:T(8,128)} async-done(((f32[384,48,128]{2,1,0:T(8,128)}), f32[24,48,128]{2,1,0:T(8,128)}) %reduce-scatter.5.cloned.1.call-update) | async-done | bytes 589840 | tf_op jit(solution)/shard_map/reduce_scatter | solution.py:90
  505.8 1.3 reduce_sum.78
  507.1 1.5 multiply_reduce_fusion
  508.6 2.7 fusion
  (18 shorter events, 0.1 us)
Async XLA Ops:
  19.1 220.0 %all-to-all-start = ((f32[16,24,48,128]{3,2,1,0:T(8,128)}), f32[16,24,48,128]{3,2,1,0:T(8,128)}, u32[]{:S(2)}, u32[]{:S(2)}) async-start(f32[16,24,48,128]{3,2,1,0:T(8,128)} %stack.2), calls=%async_computation | async-start | bytes 18874368 | tf_op jit(solution)/shard_map/all_to_all | solution.py:74
  32.6 301.7 %reduce-scatter.3.cloned.1.call-start = ((), (), s32[]{:S(2)}) async-start(), calls=%async_computation.3 | async-start | bytes 5308416 | tf_op jit(solution)/shard_map/reduce_scatter | solution.py:79
  264.9 0.7 copy-start.3
  264.9 0.7 copy-start.4
  264.9 1.1 copy-start
  264.9 1.1 copy-start.5
  264.9 74.0 %copy-start.2 = (f32[2,128,128]{2,1,0:T(8,128)S(1)}, f32[2,128,128]{2,1,0:T(8,128)}, u32[]{:S(2)}) copy-start(f32[2,128,128]{2,1,0:T(8,128)} %param.17) | copy-start | bytes 393220
  265.0 75.1 %copy-start.1 = (f32[2,128,512]{2,1,0:T(8,128)S(1)}, f32[2,128,512]{2,1,0:T(8,128)}, u32[]{:S(2)}) copy-start(f32[2,128,512]{2,1,0:T(8,128)} %param.13) | copy-start | bytes 1572868
  265.0 138.2 %all-gather.2.cloned.1.call-start = ((), (), s32[]{:S(2)}) async-start(), calls=%async_computation.4 | async-start | bytes 5308416 | tf_op jit(solution)/shard_map/all_gather | solution.py:86
  343.3 162.4 %reduce-scatter.5.cloned.1.call-start = ((), (), s32[]{:S(2)}) async-start(), calls=%async_computation.5 | async-start | bytes 10027008 | tf_op jit(solution)/shard_map/reduce_scatter | solution.py:90
Sparse Core Ops, SparseCore 0:
  265.1 69.2 reduce-scatter.2
  343.5 59.7 all-gather.1
  431.2 74.5 reduce-scatter.4
